TPU v7x, 32 devices: a 4x4x1 block of a 4x4x8 slice. The times are simulated.
32 devices in a mesh: data: 1 (over z), model: 4 (over y), stage: 8 (over x, core).
Axes of the slice: x: 4, y: 4, z: 1, core: 2. Of those that a mesh axis runs over, the one named last changes fastest.
The devices are a block of a 4x4x8 slice.
Arguments:
- inputs: bfloat16 [8, 256, 1536], P('data')
- targets: bfloat16 [8, 256, 1536], P('data')
- w_in: bfloat16 [8, 1, 1536, 6144], P('stage', None, None, 'model')
- w_out: bfloat16 [8, 1, 6144, 1536], P('stage', None, 'model')
Outputs:
- output 1: float32 [8, 1, 1536, 6144], P(('data', 'stage'), None, None, 'model')
- output 2: float32 [8, 1, 6144, 1536], P(('data', 'stage'), None, 'model')
- output 3: float32 [1], P('data')
All inputs are finite; a program needn't handle non-finite values.
Results may differ from a plain program's by a relative error of at most 0.00704361.
Values are sent between devices in bfloat16 or wider.
A program may use at most 768 MiB of HBM per device.

v0:
```python
import jax
import jax.numpy as jnp
from jax import lax
from jax.sharding import PartitionSpec as P

GELU_COEF = 0.7978845608028654
CUBIC_COEF = 0.044715


def gelu_tanh(values):
    inner_arg = GELU_COEF * (values + CUBIC_COEF * values * values * values)
    return 0.5 * values * (1.0 + jnp.tanh(inner_arg))


def gelu_slope(values):
    tanh_val = jnp.tanh(GELU_COEF * (values + CUBIC_COEF * values * values * values))
    return 0.5 * (1.0 + tanh_val) + 0.5 * values * (1.0 - tanh_val * tanh_val) * GELU_COEF * (1.0 + 3.0 * CUBIC_COEF * values * values)


def solution(mesh):
    n_stage = mesh.shape["stage"]
    down_perm = [(src_pos, src_pos + 1) for src_pos in range(n_stage - 1)]
    up_perm = [(src_pos + 1, src_pos) for src_pos in range(n_stage - 1)]

    def stage_step(inputs, targets, w_in, w_out):
        num_micro, num_tokens, model_dim = inputs.shape
        layers_here = w_in.shape[1]
        w_in_loc = w_in[0]
        w_out_loc = w_out[0]
        stage_pos = lax.axis_index("stage")
        is_last = stage_pos == n_stage - 1
        num_ticks = num_micro + n_stage - 1
        grad_scale = 1.0 / (num_micro * num_tokens * model_dim)

        def fwd_tick(state_in, tick_num):
            recv_act, loss_sum = state_in
            mb_index = tick_num - stage_pos
            first_in = lax.dynamic_index_in_dim(inputs, jnp.clip(tick_num, 0, num_micro - 1), 0, keepdims=False)
            hidden = jnp.where(stage_pos == 0, first_in, recv_act)
            saved_in = []
            saved_pre = []
            saved_act = []
            for layer_pos in range(layers_here):
                pre_act = jnp.dot(hidden, w_in_loc[layer_pos], preferred_element_type=jnp.float32).astype(jnp.bfloat16)
                act_out = gelu_tanh(pre_act.astype(jnp.float32)).astype(jnp.bfloat16)
                part_sum = jnp.dot(act_out, w_out_loc[layer_pos], preferred_element_type=jnp.float32)
                saved_in.append(hidden)
                saved_pre.append(pre_act)
                saved_act.append(act_out)
                hidden = (hidden.astype(jnp.float32) + lax.psum(part_sum, "model")).astype(jnp.bfloat16)
            tgt_mb = lax.dynamic_index_in_dim(targets, jnp.clip(mb_index, 0, num_micro - 1), 0, keepdims=False)
            out_err = hidden.astype(jnp.float32) - tgt_mb.astype(jnp.float32)
            start_grad = (out_err * grad_scale).astype(jnp.bfloat16)
            keep_loss = is_last & (mb_index >= 0) & (mb_index < num_micro)
            loss_sum = loss_sum + jnp.where(keep_loss, 0.5 * jnp.sum(out_err * out_err), 0.0)
            sent_act = lax.ppermute(hidden, "stage", down_perm)
            return (sent_act, loss_sum), (jnp.stack(saved_in), jnp.stack(saved_pre), jnp.stack(saved_act), start_grad)

        fwd_init = (jnp.zeros((num_tokens, model_dim), jnp.bfloat16), jnp.zeros((), jnp.float32))
        (last_act, loss_sum), (all_in, all_pre, all_act, all_start) = lax.scan(fwd_tick, fwd_init, jnp.arange(num_ticks))

        def bwd_tick(state_in, tick_num):
            recv_grad, acc_in, acc_out = state_in
            mb_index = tick_num - (n_stage - 1 - stage_pos)
            is_valid = (mb_index >= 0) & (mb_index < num_micro)
            save_pos = jnp.clip(mb_index + stage_pos, 0, num_ticks - 1)
            start_here = lax.dynamic_index_in_dim(all_start, save_pos, 0, keepdims=False)
            grad_h = jnp.where(is_last, start_here, recv_grad)
            grad_h = jnp.where(is_valid, grad_h, jnp.zeros_like(grad_h))
            layer_in = lax.dynamic_index_in_dim(all_in, save_pos, 0, keepdims=False)
            layer_pre = lax.dynamic_index_in_dim(all_pre, save_pos, 0, keepdims=False)
            layer_act = lax.dynamic_index_in_dim(all_act, save_pos, 0, keepdims=False)
            new_in = list(acc_in)
            new_out = list(acc_out)
            for layer_pos in reversed(range(layers_here)):
                grad_act = jnp.einsum("bd,fd->bf", grad_h, w_out_loc[layer_pos], preferred_element_type=jnp.float32).astype(jnp.bfloat16)
                grad_pre = (gelu_slope(layer_pre[layer_pos].astype(jnp.float32)) * grad_act.astype(jnp.float32)).astype(jnp.bfloat16)
                new_out[layer_pos] = new_out[layer_pos] + jnp.einsum("bf,bd->fd", layer_act[layer_pos], grad_h, preferred_element_type=jnp.float32)
                new_in[layer_pos] = new_in[layer_pos] + jnp.einsum("bd,bf->df", layer_in[layer_pos], grad_pre, preferred_element_type=jnp.float32)
                part_sum = jnp.einsum("bf,df->bd", grad_pre, w_in_loc[layer_pos], preferred_element_type=jnp.float32)
                grad_h = (grad_h.astype(jnp.float32) + lax.psum(part_sum, "model")).astype(jnp.bfloat16)
            sent_grad = lax.ppermute(grad_h, "stage", up_perm)
            return (sent_grad, tuple(new_in), tuple(new_out)), None

        zeros_in = tuple(jnp.zeros(w_in_loc.shape[1:], jnp.float32) for layer_pos in range(layers_here))
        zeros_out = tuple(jnp.zeros(w_out_loc.shape[1:], jnp.float32) for layer_pos in range(layers_here))
        bwd_init = (jnp.zeros((num_tokens, model_dim), jnp.bfloat16), zeros_in, zeros_out)
        (first_grad, acc_in, acc_out), unused_ys = lax.scan(bwd_tick, bwd_init, jnp.arange(num_ticks))
        loss_out = jnp.reshape(lax.psum(loss_sum, "stage") * grad_scale, (1,))
        return jnp.stack(acc_in)[None], jnp.stack(acc_out)[None], loss_out

    return jax.shard_map(
        stage_step,
        mesh=mesh,
        in_specs=(P("data", None, None), P("data", None, None), P("stage", None, None, "model"), P("stage", None, "model", None)),
        out_specs=(P(("data", "stage"), None, None, "model"), P(("data", "stage"), None, "model", None), P("data")),
        check_vma=False,
    )
```

profile of v0, /device:TPU:96, one launch (start us, length us, event | category | flops | bytes accessed | tf_op | source)
XLA Modules:
  0.0 2287.1 jit_solution(13111839775352409289)
XLA Ops:
  7.3 1090.6 %while.37 = (s32[]{:T(128)}, bf16[256,1536]{1,0:T(8,128)(2,1)S(1)}, f32[]{:T(128)}, bf16[15,1,256,1536]{3,2,1,0:T(8,128)(2,1)}, bf16[15,1,256,1536]{3,2,1,0:T(8,...) while((s32[]{:T(128)}, bf16[256,1536]{1,0:T(8,128)(2,1)S(1)}, ...), condition=%wide.region_3.4_spmd, body=%wide.region_0.3_spmd.sunk | while | flops 2430074880 | bytes 51120592 | solution.py:60
  19.3 47.5 %all-reduce.3.cloned.1.call-done = f32[256,1536]{1,0:T(8,128)} async-done(((f32[256,1536]{1,0:T(8,128)}), f32[256,1536]{1,0:T(8,128)}) %all-reduce.3.cloned.1.call-update) | async-done | bytes 1572880 | tf_op jit(solution)/shard_map/while/body/eval_jaxpr/psum | solution.py:50
  86.5 53.5 %all-reduce.3.cloned.1.call-done = f32[256,1536]{1,0:T(8,128)} async-done(((f32[256,1536]{1,0:T(8,128)}), f32[256,1536]{1,0:T(8,128)}) %all-reduce.3.cloned.1.call-update) | async-done | bytes 1572880 | tf_op jit(solution)/shard_map/while/body/eval_jaxpr/psum | solution.py:50
  159.6 53.4 %all-reduce.3.cloned.1.call-done = f32[256,1536]{1,0:T(8,128)} async-done(((f32[256,1536]{1,0:T(8,128)}), f32[256,1536]{1,0:T(8,128)}) %all-reduce.3.cloned.1.call-update) | async-done | bytes 1572880 | tf_op jit(solution)/shard_map/while/body/eval_jaxpr/psum | solution.py:50
  232.8 53.5 %all-reduce.3.cloned.1.call-done = f32[256,1536]{1,0:T(8,128)} async-done(((f32[256,1536]{1,0:T(8,128)}), f32[256,1536]{1,0:T(8,128)}) %all-reduce.3.cloned.1.call-update) | async-done | bytes 1572880 | tf_op jit(solution)/shard_map/while/body/eval_jaxpr/psum | solution.py:50
  305.8 53.5 %all-reduce.3.cloned.1.call-done = f32[256,1536]{1,0:T(8,128)} async-done(((f32[256,1536]{1,0:T(8,128)}), f32[256,1536]{1,0:T(8,128)}) %all-reduce.3.cloned.1.call-update) | async-done | bytes 1572880 | tf_op jit(solution)/shard_map/while/body/eval_jaxpr/psum | solution.py:50
  378.8 53.5 %all-reduce.3.cloned.1.call-done = f32[256,1536]{1,0:T(8,128)} async-done(((f32[256,1536]{1,0:T(8,128)}), f32[256,1536]{1,0:T(8,128)}) %all-reduce.3.cloned.1.call-update) | async-done | bytes 1572880 | tf_op jit(solution)/shard_map/while/body/eval_jaxpr/psum | solution.py:50
  452.0 53.5 %all-reduce.3.cloned.1.call-done = f32[256,1536]{1,0:T(8,128)} async-done(((f32[256,1536]{1,0:T(8,128)}), f32[256,1536]{1,0:T(8,128)}) %all-reduce.3.cloned.1.call-update) | async-done | bytes 1572880 | tf_op jit(solution)/shard_map/while/body/eval_jaxpr/psum | solution.py:50
  525.1 53.5 %all-reduce.3.cloned.1.call-done = f32[256,1536]{1,0:T(8,128)} async-done(((f32[256,1536]{1,0:T(8,128)}), f32[256,1536]{1,0:T(8,128)}) %all-reduce.3.cloned.1.call-update) | async-done | bytes 1572880 | tf_op jit(solution)/shard_map/while/body/eval_jaxpr/psum | solution.py:50
  598.2 53.5 %all-reduce.3.cloned.1.call-done = f32[256,1536]{1,0:T(8,128)} async-done(((f32[256,1536]{1,0:T(8,128)}), f32[256,1536]{1,0:T(8,128)}) %all-reduce.3.cloned.1.call-update) | async-done | bytes 1572880 | tf_op jit(solution)/shard_map/while/body/eval_jaxpr/psum | solution.py:50
  671.3 53.5 %all-reduce.3.cloned.1.call-done = f32[256,1536]{1,0:T(8,128)} async-done(((f32[256,1536]{1,0:T(8,128)}), f32[256,1536]{1,0:T(8,128)}) %all-reduce.3.cloned.1.call-update) | async-done | bytes 1572880 | tf_op jit(solution)/shard_map/while/body/eval_jaxpr/psum | solution.py:50
  744.4 53.4 %all-reduce.3.cloned.1.call-done = f32[256,1536]{1,0:T(8,128)} async-done(((f32[256,1536]{1,0:T(8,128)}), f32[256,1536]{1,0:T(8,128)}) %all-reduce.3.cloned.1.call-update) | async-done | bytes 1572880 | tf_op jit(solution)/shard_map/while/body/eval_jaxpr/psum | solution.py:50
  817.6 53.5 %all-reduce.3.cloned.1.call-done = f32[256,1536]{1,0:T(8,128)} async-done(((f32[256,1536]{1,0:T(8,128)}), f32[256,1536]{1,0:T(8,128)}) %all-reduce.3.cloned.1.call-update) | async-done | bytes 1572880 | tf_op jit(solution)/shard_map/while/body/eval_jaxpr/psum | solution.py:50
  890.7 53.4 %all-reduce.3.cloned.1.call-done = f32[256,1536]{1,0:T(8,128)} async-done(((f32[256,1536]{1,0:T(8,128)}), f32[256,1536]{1,0:T(8,128)}) %all-reduce.3.cloned.1.call-update) | async-done | bytes 1572880 | tf_op jit(solution)/shard_map/while/body/eval_jaxpr/psum | solution.py:50
  963.7 53.5 %all-reduce.3.cloned.1.call-done = f32[256,1536]{1,0:T(8,128)} async-done(((f32[256,1536]{1,0:T(8,128)}), f32[256,1536]{1,0:T(8,128)}) %all-reduce.3.cloned.1.call-update) | async-done | bytes 1572880 | tf_op jit(solution)/shard_map/while/body/eval_jaxpr/psum | solution.py:50
  1036.9 53.4 %all-reduce.3.cloned.1.call-done = f32[256,1536]{1,0:T(8,128)} async-done(((f32[256,1536]{1,0:T(8,128)}), f32[256,1536]{1,0:T(8,128)}) %all-reduce.3.cloned.1.call-update) | async-done | bytes 1572880 | tf_op jit(solution)/shard_map/while/body/eval_jaxpr/psum | solution.py:50
  1097.9 1163.4 %while.38 = (s32[]{:T(128)}, bf16[256,1536]{1,0:T(8,128)(2,1)S(1)}, f32[1536,1536]{1,0:T(8,128)}, f32[1536,1536]{1,0:T(8,128)}, s32[15]{0:T(128)S(1)}, /*index=5...) while((s32[]{:T(128)}, bf16[256,1536]{1,0:T(8,128)(2,1)S(1)}, ...), condition=%wide.region_6.7_spmd.clone, body=%wide.region_4.6_spmd.clone.sunk | while | flops 4852285440 | bytes 87294352 | solution.py:88
  1108.1 54.1 %all-reduce.5.cloned.1.call-done = f32[256,1536]{1,0:T(8,128)} async-done(((f32[256,1536]{1,0:T(8,128)}), f32[256,1536]{1,0:T(8,128)}) %all-reduce.5.cloned.1.call-update) | async-done | bytes 1572880 | tf_op jit(solution)/shard_map/while/body/eval_jaxpr/psum | solution.py:81
  1187.7 46.2 %all-reduce.5.cloned.1.call-done = f32[256,1536]{1,0:T(8,128)} async-done(((f32[256,1536]{1,0:T(8,128)}), f32[256,1536]{1,0:T(8,128)}) %all-reduce.5.cloned.1.call-update) | async-done | bytes 1572880 | tf_op jit(solution)/shard_map/while/body/eval_jaxpr/psum | solution.py:81
  1265.1 46.2 %all-reduce.5.cloned.1.call-done = f32[256,1536]{1,0:T(8,128)} async-done(((f32[256,1536]{1,0:T(8,128)}), f32[256,1536]{1,0:T(8,128)}) %all-reduce.5.cloned.1.call-update) | async-done | bytes 1572880 | tf_op jit(solution)/shard_map/while/body/eval_jaxpr/psum | solution.py:81
  1342.5 46.2 %all-reduce.5.cloned.1.call-done = f32[256,1536]{1,0:T(8,128)} async-done(((f32[256,1536]{1,0:T(8,128)}), f32[256,1536]{1,0:T(8,128)}) %all-reduce.5.cloned.1.call-update) | async-done | bytes 1572880 | tf_op jit(solution)/shard_map/while/body/eval_jaxpr/psum | solution.py:81
  1420.0 46.2 %all-reduce.5.cloned.1.call-done = f32[256,1536]{1,0:T(8,128)} async-done(((f32[256,1536]{1,0:T(8,128)}), f32[256,1536]{1,0:T(8,128)}) %all-reduce.5.cloned.1.call-update) | async-done | bytes 1572880 | tf_op jit(solution)/shard_map/while/body/eval_jaxpr/psum | solution.py:81
  1497.4 46.2 %all-reduce.5.cloned.1.call-done = f32[256,1536]{1,0:T(8,128)} async-done(((f32[256,1536]{1,0:T(8,128)}), f32[256,1536]{1,0:T(8,128)}) %all-reduce.5.cloned.1.call-update) | async-done | bytes 1572880 | tf_op jit(solution)/shard_map/while/body/eval_jaxpr/psum | solution.py:81
  1574.8 46.2 %all-reduce.5.cloned.1.call-done = f32[256,1536]{1,0:T(8,128)} async-done(((f32[256,1536]{1,0:T(8,128)}), f32[256,1536]{1,0:T(8,128)}) %all-reduce.5.cloned.1.call-update) | async-done | bytes 1572880 | tf_op jit(solution)/shard_map/while/body/eval_jaxpr/psum | solution.py:81
  1652.2 46.2 %all-reduce.5.cloned.1.call-done = f32[256,1536]{1,0:T(8,128)} async-done(((f32[256,1536]{1,0:T(8,128)}), f32[256,1536]{1,0:T(8,128)}) %all-reduce.5.cloned.1.call-update) | async-done | bytes 1572880 | tf_op jit(solution)/shard_map/while/body/eval_jaxpr/psum | solution.py:81
  1729.6 46.2 %all-reduce.5.cloned.1.call-done = f32[256,1536]{1,0:T(8,128)} async-done(((f32[256,1536]{1,0:T(8,128)}), f32[256,1536]{1,0:T(8,128)}) %all-reduce.5.cloned.1.call-update) | async-done | bytes 1572880 | tf_op jit(solution)/shard_map/while/body/eval_jaxpr/psum | solution.py:81
  1807.0 46.2 %all-reduce.5.cloned.1.call-done = f32[256,1536]{1,0:T(8,128)} async-done(((f32[256,1536]{1,0:T(8,128)}), f32[256,1536]{1,0:T(8,128)}) %all-reduce.5.cloned.1.call-update) | async-done | bytes 1572880 | tf_op jit(solution)/shard_map/while/body/eval_jaxpr/psum | solution.py:81
  1884.4 46.2 %all-reduce.5.cloned.1.call-done = f32[256,1536]{1,0:T(8,128)} async-done(((f32[256,1536]{1,0:T(8,128)}), f32[256,1536]{1,0:T(8,128)}) %all-reduce.5.cloned.1.call-update) | async-done | bytes 1572880 | tf_op jit(solution)/shard_map/while/body/eval_jaxpr/psum | solution.py:81
  1961.8 46.2 %all-reduce.5.cloned.1.call-done = f32[256,1536]{1,0:T(8,128)} async-done(((f32[256,1536]{1,0:T(8,128)}), f32[256,1536]{1,0:T(8,128)}) %all-reduce.5.cloned.1.call-update) | async-done | bytes 1572880 | tf_op jit(solution)/shard_map/while/body/eval_jaxpr/psum | solution.py:81
  2039.2 46.2 %all-reduce.5.cloned.1.call-done = f32[256,1536]{1,0:T(8,128)} async-done(((f32[256,1536]{1,0:T(8,128)}), f32[256,1536]{1,0:T(8,128)}) %all-reduce.5.cloned.1.call-update) | async-done | bytes 1572880 | tf_op jit(solution)/shard_map/while/body/eval_jaxpr/psum | solution.py:81
  2116.6 46.2 %all-reduce.5.cloned.1.call-done = f32[256,1536]{1,0:T(8,128)} async-done(((f32[256,1536]{1,0:T(8,128)}), f32[256,1536]{1,0:T(8,128)}) %all-reduce.5.cloned.1.call-update) | async-done | bytes 1572880 | tf_op jit(solution)/shard_map/while/body/eval_jaxpr/psum | solution.py:81
  2194.0 46.2 %all-reduce.5.cloned.1.call-done = f32[256,1536]{1,0:T(8,128)} async-done(((f32[256,1536]{1,0:T(8,128)}), f32[256,1536]{1,0:T(8,128)}) %all-reduce.5.cloned.1.call-update) | async-done | bytes 1572880 | tf_op jit(solution)/shard_map/while/body/eval_jaxpr/psum | solution.py:81
  (476 shorter events, 735.0 us)
Async XLA Ops:
  7.3 59.6 %all-reduce.3.cloned.1.call-start = ((), (), s32[]{:S(2)}) async-start(), calls=%async_computation | async-start | bytes 3145728 | tf_op jit(solution)/shard_map/while/body/eval_jaxpr/psum | solution.py:50
  74.4 65.6 %all-reduce.3.cloned.1.call-start = ((), (), s32[]{:S(2)}) async-start(), calls=%async_computation | async-start | bytes 3145728 | tf_op jit(solution)/shard_map/while/body/eval_jaxpr/psum | solution.py:50
  147.6 65.5 %all-reduce.3.cloned.1.call-start = ((), (), s32[]{:S(2)}) async-start(), calls=%async_computation | async-start | bytes 3145728 | tf_op jit(solution)/shard_map/while/body/eval_jaxpr/psum | solution.py:50
  220.7 65.5 %all-reduce.3.cloned.1.call-start = ((), (), s32[]{:S(2)}) async-start(), calls=%async_computation | async-start | bytes 3145728 | tf_op jit(solution)/shard_map/while/body/eval_jaxpr/psum | solution.py:50
  293.7 65.5 %all-reduce.3.cloned.1.call-start = ((), (), s32[]{:S(2)}) async-start(), calls=%async_computation | async-start | bytes 3145728 | tf_op jit(solution)/shard_map/while/body/eval_jaxpr/psum | solution.py:50
  366.8 65.5 %all-reduce.3.cloned.1.call-start = ((), (), s32[]{:S(2)}) async-start(), calls=%async_computation | async-start | bytes 3145728 | tf_op jit(solution)/shard_map/while/body/eval_jaxpr/psum | solution.py:50
  439.9 65.5 %all-reduce.3.cloned.1.call-start = ((), (), s32[]{:S(2)}) async-start(), calls=%async_computation | async-start | bytes 3145728 | tf_op jit(solution)/shard_map/while/body/eval_jaxpr/psum | solution.py:50
  513.0 65.6 %all-reduce.3.cloned.1.call-start = ((), (), s32[]{:S(2)}) async-start(), calls=%async_computation | async-start | bytes 3145728 | tf_op jit(solution)/shard_map/while/body/eval_jaxpr/psum | solution.py:50
  586.1 65.5 %all-reduce.3.cloned.1.call-start = ((), (), s32[]{:S(2)}) async-start(), calls=%async_computation | async-start | bytes 3145728 | tf_op jit(solution)/shard_map/while/body/eval_jaxpr/psum | solution.py:50
  659.2 65.5 %all-reduce.3.cloned.1.call-start = ((), (), s32[]{:S(2)}) async-start(), calls=%async_computation | async-start | bytes 3145728 | tf_op jit(solution)/shard_map/while/body/eval_jaxpr/psum | solution.py:50
  732.3 65.5 %all-reduce.3.cloned.1.call-start = ((), (), s32[]{:S(2)}) async-start(), calls=%async_computation | async-start | bytes 3145728 | tf_op jit(solution)/shard_map/while/body/eval_jaxpr/psum | solution.py:50
  805.4 65.6 %all-reduce.3.cloned.1.call-start = ((), (), s32[]{:S(2)}) async-start(), calls=%async_computation | async-start | bytes 3145728 | tf_op jit(solution)/shard_map/while/body/eval_jaxpr/psum | solution.py:50
  878.6 65.5 %all-reduce.3.cloned.1.call-start = ((), (), s32[]{:S(2)}) async-start(), calls=%async_computation | async-start | bytes 3145728 | tf_op jit(solution)/shard_map/while/body/eval_jaxpr/psum | solution.py:50
  951.6 65.5 %all-reduce.3.cloned.1.call-start = ((), (), s32[]{:S(2)}) async-start(), calls=%async_computation | async-start | bytes 3145728 | tf_op jit(solution)/shard_map/while/body/eval_jaxpr/psum | solution.py:50
  1024.7 65.6 %all-reduce.3.cloned.1.call-start = ((), (), s32[]{:S(2)}) async-start(), calls=%async_computation | async-start | bytes 3145728 | tf_op jit(solution)/shard_map/while/body/eval_jaxpr/psum | solution.py:50
  1098.0 64.2 %all-reduce.5.cloned.1.call-start = ((), (), s32[]{:S(2)}) async-start(), calls=%async_computation.1 | async-start | bytes 3145728 | tf_op jit(solution)/shard_map/while/body/eval_jaxpr/psum | solution.py:81
  1177.7 56.3 %all-reduce.5.cloned.1.call-start = ((), (), s32[]{:S(2)}) async-start(), calls=%async_computation.1 | async-start | bytes 3145728 | tf_op jit(solution)/shard_map/while/body/eval_jaxpr/psum | solution.py:81
  1255.1 56.3 %all-reduce.5.cloned.1.call-start = ((), (), s32[]{:S(2)}) async-start(), calls=%async_computation.1 | async-start | bytes 3145728 | tf_op jit(solution)/shard_map/while/body/eval_jaxpr/psum | solution.py:81
  1313.0 19.5 collective-permute-start.1
  1332.5 56.3 %all-reduce.5.cloned.1.call-start = ((), (), s32[]{:S(2)}) async-start(), calls=%async_computation.1 | async-start | bytes 3145728 | tf_op jit(solution)/shard_map/while/body/eval_jaxpr/psum | solution.py:81
  1409.9 56.3 %all-reduce.5.cloned.1.call-start = ((), (), s32[]{:S(2)}) async-start(), calls=%async_computation.1 | async-start | bytes 3145728 | tf_op jit(solution)/shard_map/while/body/eval_jaxpr/psum | solution.py:81
  1467.8 19.5 collective-permute-start.1
  1487.3 56.3 %all-reduce.5.cloned.1.call-start = ((), (), s32[]{:S(2)}) async-start(), calls=%async_computation.1 | async-start | bytes 3145728 | tf_op jit(solution)/shard_map/while/body/eval_jaxpr/psum | solution.py:81
  1564.7 56.3 %all-reduce.5.cloned.1.call-start = ((), (), s32[]{:S(2)}) async-start(), calls=%async_computation.1 | async-start | bytes 3145728 | tf_op jit(solution)/shard_map/while/body/eval_jaxpr/psum | solution.py:81
  1642.1 56.3 %all-reduce.5.cloned.1.call-start = ((), (), s32[]{:S(2)}) async-start(), calls=%async_computation.1 | async-start | bytes 3145728 | tf_op jit(solution)/shard_map/while/body/eval_jaxpr/psum | solution.py:81
  1719.5 56.3 %all-reduce.5.cloned.1.call-start = ((), (), s32[]{:S(2)}) async-start(), calls=%async_computation.1 | async-start | bytes 3145728 | tf_op jit(solution)/shard_map/while/body/eval_jaxpr/psum | solution.py:81
  1796.9 56.3 %all-reduce.5.cloned.1.call-start = ((), (), s32[]{:S(2)}) async-start(), calls=%async_computation.1 | async-start | bytes 3145728 | tf_op jit(solution)/shard_map/while/body/eval_jaxpr/psum | solution.py:81
  1874.3 56.3 %all-reduce.5.cloned.1.call-start = ((), (), s32[]{:S(2)}) async-start(), calls=%async_computation.1 | async-start | bytes 3145728 | tf_op jit(solution)/shard_map/while/body/eval_jaxpr/psum | solution.py:81
  1951.7 56.3 %all-reduce.5.cloned.1.call-start = ((), (), s32[]{:S(2)}) async-start(), calls=%async_computation.1 | async-start | bytes 3145728 | tf_op jit(solution)/shard_map/while/body/eval_jaxpr/psum | solution.py:81
  2029.2 56.3 %all-reduce.5.cloned.1.call-start = ((), (), s32[]{:S(2)}) async-start(), calls=%async_computation.1 | async-start | bytes 3145728 | tf_op jit(solution)/shard_map/while/body/eval_jaxpr/psum | solution.py:81
  2106.6 56.3 %all-reduce.5.cloned.1.call-start = ((), (), s32[]{:S(2)}) async-start(), calls=%async_computation.1 | async-start | bytes 3145728 | tf_op jit(solution)/shard_map/while/body/eval_jaxpr/psum | solution.py:81
  2184.0 56.3 %all-reduce.5.cloned.1.call-start = ((), (), s32[]{:S(2)}) async-start(), calls=%async_computation.1 | async-start | bytes 3145728 | tf_op jit(solution)/shard_map/while/body/eval_jaxpr/psum | solution.py:81
  (88 other events, 670.9 us)
Sparse Core Ops, SparseCore 0:
  18.9 47.9 all-reduce.2
  86.1 53.8 all-reduce.2
  159.2 53.8 all-reduce.2
  232.3 53.8 all-reduce.2
  305.4 53.8 all-reduce.2
  378.4 53.8 all-reduce.2
  451.5 53.8 all-reduce.2
  524.6 53.8 all-reduce.2
  597.7 53.8 all-reduce.2
  670.8 53.8 all-reduce.2
  744.0 53.8 all-reduce.2
  817.1 53.8 all-reduce.2
  890.2 53.8 all-reduce.2
  963.3 53.8 all-reduce.2
  1036.4 53.8 all-reduce.2
  1108.2 53.8 all-reduce.4
  1187.9 46.0 all-reduce.4
  1265.3 46.0 all-reduce.4
  1342.7 46.0 all-reduce.4
  1420.1 46.0 all-reduce.4
  1497.5 46.0 all-reduce.4
  1574.9 46.0 all-reduce.4
  1652.3 46.0 all-reduce.4
  1729.7 46.0 all-reduce.4
  1807.1 46.0 all-reduce.4
  1884.5 46.0 all-reduce.4
  1961.9 46.0 all-reduce.4
  2039.3 46.0 all-reduce.4
  2116.7 46.0 all-reduce.4
  2194.1 46.0 all-reduce.4
where the time goes:
time: 2290 us
  waiting for transfers between devices  1500 us (66%)
  matrix products  494 us (22%)
  other arithmetic  156 us (7%)
  starting transfers between devices  47.8 us (2%)
  loops' own time  39.1 us (2%)
    psum x15, waiting for transfers between devices, fwd_tick(): lax.psum(part_sum, 'model')  796 us
    psum x15, waiting for transfers between devices, bwd_tick(): lax.psum(part_sum, 'model')  701 us
    dot_general x15, matrix products, bwd_tick(): jnp.einsum('bd,bf->df', layer_in[layer_pos], grad_pre, preferred_element_...  134 us
    dot_general x15, matrix products, bwd_tick(): jnp.einsum('bf,bd->fd', layer_act[layer_pos], grad_h, preferred_element_t...  134 us
    dynamic_update_slice x30, other arithmetic, stage_step(): lax.scan(fwd_tick, fwd_init, jnp.arange(num_ticks))  79 us
    dot_general x15, matrix products, fwd_tick(): jnp.dot(hidden, w_in_loc[layer_pos], preferred_element_type=jnp.float32)  77.8 us
    dot_general x15, matrix products, bwd_tick(): jnp.einsum('bd,fd->bf', grad_h, w_out_loc[layer_pos], preferred_element_t...  69.8 us
  transfers between devices with their start and end apart: 60, of which 30 were waited for; matrix products, arithmetic and copies ran while one was open for 13% of the time, Pallas kernels for 0%

commit v1 on v0

v1 whole, which is shorter than its diff:
```python
import functools

import jax
import jax.numpy as jnp
from jax import lax
from jax.experimental import pallas as pl
from jax.experimental.pallas import tpu as pltpu
from jax.sharding import PartitionSpec as P

GELU_COEF = 0.7978845608028654
CUBIC_COEF = 0.044715
MESH = pl.DeviceIdType.MESH
F32 = jnp.float32
BF16 = jnp.bfloat16

TOKENS = 128
SLOTS = 4
NT = (((1,), (1,)), ((), ()))
TN = (((0,), (0,)), ((), ()))


def dot(a, b, dims=(((1,), (0,)), ((), ()))):
    return lax.dot_general(a, b, dims, preferred_element_type=F32)


def kernel(n_stage, x_hbm, t_hbm, w1_hbm, w2_hbm, dw1_hbm, dw2_hbm, loss_ref,
           w1, w2, dw1, dw2, xs, us, es, ab, gb, ps, rs, outs, tgt, err_acc, ltile,
           load_sem, x_sem, e_sem, r_sem, p_sem, o_sem, l_sem, chain_sem, store_sem):
    n_model = 4
    num, _, rows, width = xs.shape
    tokens = n_model * rows
    hidden = w1.shape[1]
    half = width // 2
    tile = min(512, hidden)
    scale = 1.0 / (num * tokens * width)
    s = lax.axis_index("stage")
    d = lax.axis_index("model")
    right = lax.rem(d + 1, n_model)
    left = lax.rem(d + 3, n_model)
    far = lax.rem(d + 2, n_model)
    first = s == 0
    last = s == n_stage - 1
    up = lax.rem(s + 1, n_stage)
    down = lax.rem(s + n_stage - 1, n_stage)

    def peer(k):
        return lax.rem(d + k, n_model)

    def send(src, dst, ssem, rsem, model, stage):
        return pltpu.make_async_remote_copy(
            src_ref=src, dst_ref=dst, send_sem=ssem, recv_sem=rsem,
            device_id={"model": model, "stage": stage}, device_id_type=MESH)

    def got(ref, sem):
        send(ref, ref, sem, sem, right, s).wait_recv()

    def sent(ref, sem):
        send(ref, ref, sem, sem, right, s).wait_send()

    load_w1 = pltpu.make_async_copy(w1_hbm, w1, load_sem.at[0])
    load_w2 = pltpu.make_async_copy(w2_hbm, w2, load_sem.at[1])
    load_x = pltpu.make_async_copy(x_hbm, xs, load_sem.at[2])
    load_t = pltpu.make_async_copy(t_hbm.at[:, d], tgt, load_sem.at[3])

    @pl.when(first)
    def _():
        load_x.start()

    load_w1.start()
    load_w2.start()

    @pl.when(last)
    def _():
        load_t.start()

    barrier = pltpu.get_barrier_semaphore()
    for k in range(1, n_model):
        pl.semaphore_signal(barrier, inc=1, device_id={"model": peer(k), "stage": s}, device_id_type=MESH)
    for k in range(n_model):
        pl.semaphore_signal(barrier, inc=1, device_id={"model": peer(k), "stage": up}, device_id_type=MESH)
        pl.semaphore_signal(barrier, inc=1, device_id={"model": peer(k), "stage": down}, device_id_type=MESH)

    def zero(i, c):
        r = pl.ds(pl.multiple_of(i * 64, 64), 64)
        dw1[r, :] = jnp.zeros((64, dw1.shape[1]), F32)
        return c

    lax.fori_loop(0, dw1.shape[0] // 64, zero, 0)

    def zero2(i, c):
        r = pl.ds(pl.multiple_of(i * 64, 64), 64)
        dw2[r, :] = jnp.zeros((64, dw2.shape[1]), F32)
        return c

    lax.fori_loop(0, dw2.shape[0] // 64, zero2, 0)
    err_acc[...] = jnp.zeros_like(err_acc)
    pl.semaphore_wait(barrier, 3 * n_model - 1)

    @pl.when(first)
    def _():
        load_x.wait()

    load_w1.wait()
    load_w2.wait()

    @pl.when(last)
    def _():
        load_t.wait()

    def exchange(slot):
        def step(h, o, k, dev):
            return send(ps.at[h, o], rs.at[slot, k], p_sem.at[k], r_sem.at[slot, k], dev, s)

        return (
            step(0, far, 0, right), step(1, far, 1, left),
            step(1, right, 2, right), step(0, left, 3, left),
            step(0, right, 4, right), step(1, left, 5, left),
        )

    def relay_sums(slot):
        ex = exchange(slot)
        got(rs.at[slot, 0], r_sem.at[slot, 0])
        ps[0, right] += rs[slot, 0]
        ex[4].start()
        got(rs.at[slot, 1], r_sem.at[slot, 1])
        ps[1, left] += rs[slot, 1]
        ex[5].start()

    def final_sums(slot, base):
        for k in (2, 3, 4, 5):
            got(rs.at[slot, k], r_sem.at[slot, k])
        h0 = base[:, :half].astype(F32) + (ps[0, d] + rs[slot, 4] + rs[slot, 3])
        h1 = base[:, half:].astype(F32) + (ps[1, d] + rs[slot, 2] + rs[slot, 5])
        return h0.astype(BF16), h1.astype(BF16)

    def sums_sent():
        for k in range(6):
            sent(ps.at[0, 0], p_sem.at[k])

    def fwd(i, c):
        slot = lax.rem(i, SLOTS)

        @pl.when(jnp.logical_not(first))
        def _():
            got(xs.at[i], x_sem.at[i])

        xm = xs[i].reshape(tokens, width)
        for j in range(hidden // tile):
            cols = slice(j * tile, (j + 1) * tile)
            u = dot(xm, w1[:, cols]).astype(BF16)
            us[i, :, cols] = u
            uf = u.astype(F32)
            tau = jnp.tanh(GELU_COEF * (uf + CUBIC_COEF * uf * uf * uf))
            ab[:, cols] = (0.5 * uf * (1.0 + tau)).astype(BF16)
        am = ab[...]
        ex = exchange(slot)
        ps[0] = dot(am, w2[:, :half]).reshape(n_model, rows, half)
        ex[0].start()
        ex[3].start()
        ps[1] = dot(am, w2[:, half:]).reshape(n_model, rows, half)
        ex[1].start()
        ex[2].start()
        relay_sums(slot)
        h0, h1 = final_sums(slot, xs[i, d])

        @pl.when(jnp.logical_not(last))
        def _():
            outs[i, :, :half] = h0
            outs[i, :, half:] = h1
            for k in (2, 1, 3, 0):
                send(outs.at[i], xs.at[i, d], o_sem.at[k], x_sem.at[i], peer(k), up).start()

        @pl.when(last)
        def _():
            for h, v in ((0, h0), (1, h1)):
                cols = slice(h * half, (h + 1) * half)
                err = v.astype(F32) - tgt[i, :, cols].astype(F32)
                es[i, d, :, cols] = (err * scale).astype(BF16)
                err_acc[:, cols] += err * err
            for k in (2, 1, 3):
                send(es.at[i, d], es.at[i, d], o_sem.at[k], e_sem.at[i], peer(k), s).start()

        sums_sent()
        return c

    lax.fori_loop(0, num, fwd, 0)

    for k in (1, 2, 3):
        sent(outs, o_sem.at[k])

    @pl.when(jnp.logical_not(last))
    def _():
        sent(outs, o_sem.at[0])

    def bwd(i, c):
        slot = lax.rem(i, SLOTS)

        @pl.when(last)
        def _():
            got(es.at[i, pl.ds(0, n_model - 1)], e_sem.at[i])

        @pl.when(jnp.logical_not(last))
        def _():
            got(es.at[i], e_sem.at[i])

        em = es[i].reshape(tokens, width)
        for j in range(hidden // tile):
            cols = slice(j * tile, (j + 1) * tile)
            q = dot(em, w2[cols, :], NT).astype(BF16).astype(F32)
            uf = us[i, :, cols].astype(F32)
            sq = uf * uf
            tau = jnp.tanh(GELU_COEF * (uf + CUBIC_COEF * uf * sq))
            slope = 0.5 * (1.0 + tau) + 0.5 * uf * (1.0 - tau * tau) * GELU_COEF * (1.0 + 3.0 * CUBIC_COEF * sq)
            gb[:, cols] = (slope * q).astype(BF16)
            ab[:, cols] = (0.5 * uf * (1.0 + tau)).astype(BF16)

        @pl.when(jnp.logical_not(first))
        def _():
            gm = gb[...]
            ex = exchange(slot)
            ps[0] = dot(gm, w1[:half, :], NT).reshape(n_model, rows, half)
            ex[0].start()
            ex[3].start()
            ps[1] = dot(gm, w1[half:, :], NT).reshape(n_model, rows, half)
            ex[1].start()
            ex[2].start()

        for j in range(hidden // tile):
            r = slice(j * tile, (j + 1) * tile)
            dw2[r, :] += dot(ab[:, r], em, TN)

        @pl.when(jnp.logical_not(first))
        def _():
            relay_sums(slot)

        gm = gb[...]
        for j in range(width // tile):
            r = slice(j * tile, (j + 1) * tile)
            xt = xs[i, :, :, r].reshape(tokens, tile)
            dw1[r, :] += dot(xt, gm, TN)

        @pl.when(jnp.logical_not(first))
        def _():
            h0, h1 = final_sums(slot, es[i, d])
            outs[i, :, :half] = h0
            outs[i, :, half:] = h1
            for k in (2, 1, 3, 0):
                send(outs.at[i], es.at[i, d], o_sem.at[k], e_sem.at[i], peer(k), down).start()
            sums_sent()

        return c

    lax.fori_loop(0, num, bwd, 0)

    store1 = pltpu.make_async_copy(dw1, dw1_hbm, store_sem.at[0])
    store2 = pltpu.make_async_copy(dw2, dw2_hbm, store_sem.at[1])
    store1.start()
    store2.start()

    @pl.when(last)
    def _():
        ltile[d] = jnp.full(ltile.shape[1:], 0.5 * jnp.sum(err_acc[...]), F32)
        for k in (2, 1, 3):
            send(ltile.at[d], ltile.at[d], l_sem.at[k], l_sem.at[n_model], peer(k), s).start()
        got(ltile.at[pl.ds(0, n_model - 1)], l_sem.at[n_model])
        ltile[n_model] = ltile[0] + ltile[1] + ltile[2] + ltile[3]
        for k in (1, 2, 3):
            sent(ltile.at[0], l_sem.at[k])

    @pl.when(jnp.logical_not(last))
    def _():
        got(ltile.at[n_model], chain_sem.at[0])

    @pl.when(jnp.logical_not(first))
    def _():
        chain = send(ltile.at[n_model], ltile.at[n_model], chain_sem.at[1], chain_sem.at[0], d, down)
        chain.start()
        for k in (0, 1, 2, 3):
            sent(outs, o_sem.at[k])
        chain.wait_send()

    loss_ref[...] = ltile[n_model] * scale
    store1.wait()
    store2.wait()


def run_group(n_stage, tokens, x, t, w1, w2):
    num, n_model, rows, width = x.shape
    hidden = w1.shape[1]
    half = width // 2
    any_spec = pl.BlockSpec(memory_space=pl.ANY)
    vmem = pltpu.VMEM
    dma = pltpu.SemaphoreType.DMA
    flops = 12 * num * tokens * width * hidden
    return pl.pallas_call(
        functools.partial(kernel, n_stage),
        out_shape=(
            jax.ShapeDtypeStruct(w1.shape, F32),
            jax.ShapeDtypeStruct(w2.shape, F32),
            jax.ShapeDtypeStruct((8, 128), F32),
        ),
        in_specs=[any_spec] * 4,
        out_specs=(any_spec, any_spec, pl.BlockSpec(memory_space=vmem)),
        scratch_shapes=[
            vmem(w1.shape, BF16),
            vmem(w2.shape, BF16),
            vmem(w1.shape, F32),
            vmem(w2.shape, F32),
            vmem(x.shape, BF16),
            vmem((num, tokens, hidden), BF16),
            vmem(x.shape, BF16),
            vmem((tokens, hidden), BF16),
            vmem((tokens, hidden), BF16),
            vmem((2, n_model, rows, half), F32),
            vmem((SLOTS, 6, rows, half), F32),
            vmem((num, rows, width), BF16),
            vmem((num, rows, width), BF16),
            vmem((rows, width), F32),
            vmem((n_model + 1, 8, 128), F32),
            dma((4,)),
            dma((num,)),
            dma((num,)),
            dma((SLOTS, 6)),
            dma((6,)),
            dma((n_model,)),
            dma((n_model + 1,)),
            dma((2,)),
            dma((2,)),
        ],
        compiler_params=pltpu.CompilerParams(
            collective_id=0, has_side_effects=True, vmem_limit_bytes=67043328
        ),
        cost_estimate=pl.CostEstimate(flops=flops, bytes_accessed=60 * width * hidden // 4, transcendentals=0),
        name="pipeline_step",
    )(x, t, w1, w2)


def solution(mesh):
    n_stage = mesh.shape["stage"]
    n_model = mesh.shape["model"]

    def stage_step(inputs, targets, w_in, w_out):
        width = inputs.shape[-1]
        total = inputs.shape[0] * inputs.shape[1]
        num = total // TOKENS
        shape = (num, n_model, TOKENS // n_model, width)
        dw1, dw2, loss = run_group(
            n_stage, TOKENS, inputs.reshape(shape), targets.reshape(shape), w_in[0, 0], w_out[0, 0])
        return dw1[None, None], dw2[None, None], loss[0, :1]

    return jax.shard_map(
        stage_step,
        mesh=mesh,
        in_specs=(P("data", None, None), P("data", None, None), P("stage", None, None, "model"), P("stage", None, "model", None)),
        out_specs=(P(("data", "stage"), None, None, "model"), P(("data", "stage"), None, "model", None), P("data")),
        check_vma=False,
    )
```

time: 2290 us -> 734 us (0.32)
  waiting for transfers between devices: 1500 us -> 0 us
  Pallas kernels: 0 us -> 720 us
  matrix products: 494 us -> 0 us
  other arithmetic: 156 us -> 0 us
  starting transfers between devices: 47.8 us -> 0 us
  loops' own time: 39.1 us -> 0 us
    psum x30 -> x0, waiting for transfers between devices: 1500 us -> none  [the longest x15 796 us: fwd_tick(): lax.psum(part_sum, 'model')]
    pallas_call x0 -> x1, Pallas kernels: none -> 720 us  [run_group(): pl.pallas_call(functools.partial(kernel, n_stage), out_shape=(jax.ShapeDt...]
    dot_general x90 -> x0, matrix products: 494 us -> none  [the longest x15 134 us: bwd_tick(): jnp.einsum('bd,bf->df', layer_in[layer_pos], grad_pre, preferred_element_...]
    dynamic_update_slice x30 -> x0, other arithmetic: 79 us -> none  [stage_step(): lax.scan(fwd_tick, fwd_init, jnp.arange(num_ticks))]
    ppermute x30 -> x0, starting transfers between devices: 46.8 us -> none  [the longest x15 27.1 us: fwd_tick(): sent_act = lax.ppermute(hidden, 'stage', down_perm)]
    another operation x2 -> x0, loops' own time: 39.1 us -> none  [the longest x1 27.6 us: stage_step(): lax.scan(fwd_tick, fwd_init, jnp.arange(num_ticks))]
    reduce_sum x15 -> x0, other arithmetic: 32.3 us -> none  [fwd_tick(): jnp.sum(out_err * out_err)]
    convert_element_type x15 -> x0, other arithmetic: 23.8 us -> none  [bwd_tick(): (grad_h.astype(jnp.float32) + lax.psum(part_sum, 'model')).astype(jnp.bfl...]
  transfers between devices with their start and end apart: 60 -> 0, of which waited for: 30 -> 0; matrix products, arithmetic and copies ran while one was open for 13% -> 0% of each run, Pallas kernels for 0% -> 0%
where the time goes in v1:
time: 734 us
  Pallas kernels  720 us (98%)
  local copies, waits for them, and re-layouts  13.5 us (2%)
    pallas_call x1, Pallas kernels, run_group(): pl.pallas_call(functools.partial(kernel, n_stage), out_shape=(jax.ShapeDt...  720 us

profile of v1, /device:TPU:96, one launch (start us, length us, event | category | flops | bytes accessed | tf_op | source)
XLA Modules:
  0.0 734.3 jit_solution(6482219077780551865)
XLA Ops:
  0.6 720.1 %pipeline_step.1 = (f32[1536,1536]{1,0:T(8,128)}, f32[1536,1536]{1,0:T(8,128)}, f32[8,128]{1,0:T(8,128)}) custom-call(bf16[16,4,32,1536]{3,2,1,0:T(8,128)(2,1)} %bitcast.9, bf16[16,4,32,1536]{3,2,1,0:T(8,128)(2,1)} %bitcast.10, bf16[1536,1536]{1,0:T(8,128)(2,1)} %bitcast.11, bf16[1536,1536]{1,0:T(8,128)(2,1)} %bitcast.12), custom_call_target="tpu_custom_call" | custom-call | flops 57982058496 | bytes 35389440 | tf_op jit(solution)/shard_map/pipeline_step/pallas_call | solution.py:295
  720.8 1.2 slice.3
  721.9 0.0 copy-start
  721.9 8.6 %copy.9 = f32[1,1,1536,1536]{3,2,1,0:T(8,128)} copy(f32[1,1,1536,1536]{3,2,1,0:T(8,128)} %bitcast.8) | data formatting | bytes 18874368
  730.6 0.0 copy-done
  730.6 3.7 copy.10
Async XLA Ops:
  721.9 8.6 %copy-start = (f32[1536,1536]{1,0:T(8,128)S(1)}, f32[1536,1536]{1,0:T(8,128)}, u32[]{:S(2)}) copy-start(f32[1536,1536]{1,0:T(8,128)} %get-tuple-element.7) | copy-start | bytes 28311556

commit v2 on v1

v2 whole, which is shorter than its diff:
```python
import functools

import jax
import jax.numpy as jnp
from jax import lax
from jax.experimental import pallas as pl
from jax.experimental.pallas import tpu as pltpu
from jax.sharding import PartitionSpec as P

GELU_COEF = 0.7978845608028654
CUBIC_COEF = 0.044715
MESH = pl.DeviceIdType.MESH
F32 = jnp.float32
BF16 = jnp.bfloat16

TOKENS = 64
UNIT = 2
SLOTS = 2 * UNIT
AHEAD = (22, 19, 16, 13, 10, 7, 4, 1)
ORDER = (("A", 0, 0), ("T", 0, 0), ("E5", 1, 1), ("E4", 0, 0), ("A", 1, 0), ("E5", 0, 0), ("G2", 1, 0), ("G1", 1, 0), ("E4", 1, 0))
TN = (((0,), (0,)), ((), ()))


def dot(a, b, dims=(((1,), (0,)), ((), ()))):
    return lax.dot_general(a, b, dims, preferred_element_type=F32)


def kernel(n_stage, x_hbm, t_hbm, w1_hbm, w2_hbm, dw1_hbm, dw2_hbm, loss_ref,
           w1, w2, w1t, w2t, dw1, dw2, xs, us, es, ab, gb, ps, rs, outs, err_acc, ltile,
           load_sem, in_sem, r_sem, p_sem, o_sem, l_sem, chain_sem, store_sem):
    n_model = 4
    num, _, rows, width = xs.shape
    tokens = n_model * rows
    hidden = w1.shape[1]
    half = width // 2
    tile = min(512, hidden)
    scale = 1.0 / (num * tokens * width)
    s = lax.axis_index("stage")
    d = lax.axis_index("model")
    right = lax.rem(d + 1, n_model)
    left = lax.rem(d + 3, n_model)
    far = lax.rem(d + 2, n_model)
    first = s == 0
    last = s == n_stage - 1
    up = lax.rem(s + 1, n_stage)
    down = lax.rem(s + n_stage - 1, n_stage)
    ahead = jnp.int32(0)
    for k in range(n_stage):
        ahead = jnp.where(s == k, AHEAD[len(AHEAD) - n_stage + k], ahead)
    acts = (xs, es)

    def peer(k):
        return lax.rem(d + k, n_model)

    def send(src, dst, ssem, rsem, model, stage):
        return pltpu.make_async_remote_copy(
            src_ref=src, dst_ref=dst, send_sem=ssem, recv_sem=rsem,
            device_id={"model": model, "stage": stage}, device_id_type=MESH)

    def got(ref, sem):
        send(ref, ref, sem, sem, right, s).wait_recv()

    def sent(ref, sem):
        send(ref, ref, sem, sem, right, s).wait_send()

    units = num // UNIT
    tgt = outs.at[0]
    load_w1 = pltpu.make_async_copy(w1_hbm, w1, load_sem.at[0])
    load_w2 = pltpu.make_async_copy(w2_hbm, w2, load_sem.at[1])
    load_x0 = pltpu.make_async_copy(x_hbm.at[pl.ds(0, UNIT)], xs.at[pl.ds(0, UNIT)], load_sem.at[2])
    load_x1 = pltpu.make_async_copy(
        x_hbm.at[pl.ds(UNIT, num - UNIT)], xs.at[pl.ds(UNIT, num - UNIT)], load_sem.at[3])
    load_t = pltpu.make_async_copy(t_hbm.at[:, d], tgt, load_sem.at[4])

    @pl.when(first)
    def _():
        load_x0.start()

    load_w1.start()
    load_w2.start()

    @pl.when(first)
    def _():
        load_x1.start()

    @pl.when(last)
    def _():
        load_t.start()

    barrier = pltpu.get_barrier_semaphore()
    for k in range(1, n_model):
        pl.semaphore_signal(barrier, inc=1, device_id={"model": peer(k), "stage": s}, device_id_type=MESH)
    for k in range(n_model):
        pl.semaphore_signal(barrier, inc=1, device_id={"model": peer(k), "stage": up}, device_id_type=MESH)
        pl.semaphore_signal(barrier, inc=1, device_id={"model": peer(k), "stage": down}, device_id_type=MESH)

    def zero(i, c):
        r = pl.ds(pl.multiple_of(i * 64, 64), 64)
        dw1[r, :] = jnp.zeros((64, dw1.shape[1]), F32)
        return c

    lax.fori_loop(0, dw1.shape[0] // 64, zero, 0)

    def zero2(i, c):
        r = pl.ds(pl.multiple_of(i * 64, 64), 64)
        dw2[r, :] = jnp.zeros((64, dw2.shape[1]), F32)
        return c

    lax.fori_loop(0, dw2.shape[0] // 64, zero2, 0)
    err_acc[...] = jnp.zeros_like(err_acc)
    pl.semaphore_wait(barrier, 3 * n_model - 1)

    pieces = hidden // 128
    assert width == hidden
    lazy = ahead > pieces

    def transpose(c):
        r = pl.ds(pl.multiple_of(c * 128, 128), 128)
        w2t[:, r] = w2[r, :].T
        w1t[:, r] = w1[r, :].T

    @pl.when(jnp.logical_not(lazy))
    def _():
        load_w1.wait()
        load_w2.wait()

        def piece(c, carry):
            transpose(c)
            return carry

        lax.fori_loop(0, pieces, piece, 0)

    @pl.when(last)
    def _():
        load_t.wait()

    def part(f, i, k):
        h, o, dev = ((0, far, right), (1, far, left), (1, right, right), (0, left, left), (0, right, right), (1, left, left))[k]
        b = lax.rem(i, UNIT)
        slot = lax.rem(i, SLOTS)
        return send(ps.at[f, h, b, o], rs.at[f, slot, k], p_sem.at[f, b, k], r_sem.at[f, slot, k], dev, s)

    def sums_sent(f, b):
        for k in range(6):
            sent(ps.at[0, 0, 0, 0], p_sem.at[f, b, k])

    def products(f, u, mat, weight):
        steps = [u * UNIT + k for k in range(UNIT)]

        @pl.when(u >= 1)
        def _():
            for k in range(UNIT):
                sums_sent(f, k)

        for h, kinds in ((0, (0,)), (1, (1, 2, 3))):
            ps[f, h] = weight(mat, h).reshape(UNIT, n_model, rows, half)
            for k in kinds:
                for i in steps:
                    part(f, i, k).start()

    def relay_sums(f, i):
        b = lax.rem(i, UNIT)
        slot = lax.rem(i, SLOTS)
        got(rs.at[f, slot, 0], r_sem.at[f, slot, 0])
        ps[f, 0, b, right] += rs[f, slot, 0]
        part(f, i, 4).start()
        got(rs.at[f, slot, 1], r_sem.at[f, slot, 1])
        ps[f, 1, b, left] += rs[f, slot, 1]
        part(f, i, 5).start()

    def final_sums(f, i):
        b = lax.rem(i, UNIT)
        slot = lax.rem(i, SLOTS)
        for k in (2, 3, 4, 5):
            got(rs.at[f, slot, k], r_sem.at[f, slot, k])
        base = acts[f][i, d]
        h0 = base[:, :half].astype(F32) + (ps[f, 0, b, d] + rs[f, slot, 4] + rs[f, slot, 3])
        h1 = base[:, half:].astype(F32) + (ps[f, 1, b, d] + rs[f, slot, 2] + rs[f, slot, 5])
        return h0.astype(BF16), h1.astype(BF16)

    def spread(f, i, src, stage, sender, here):
        dst = acts[f].at[i, d]
        for k in (2, 1, 3) if here else (2, 1, 3, 0):
            send(src, dst, o_sem.at[sender, k], in_sem.at[f, i], peer(k), stage).start()

    def arrived(f, i):
        if f:
            @pl.when(last)
            def _():
                got(es.at[i, pl.ds(0, n_model - 1)], in_sem.at[f, i])

            @pl.when(jnp.logical_not(last))
            def _():
                got(es.at[i], in_sem.at[f, i])
        else:
            got(xs.at[i], in_sem.at[f, i])

    def unit_rows(ref, u):
        return ref[pl.ds(u * UNIT, UNIT)].reshape(UNIT * tokens, width)

    def fwd(u):
        @pl.when(jnp.logical_not(first))
        def _():
            for k in range(UNIT):
                arrived(0, u * UNIT + k)

        @pl.when(jnp.logical_and(first, u <= 1))
        def _():
            @pl.when(u == 0)
            def _():
                load_x0.wait()

            @pl.when(u == 1)
            def _():
                load_x1.wait()

        start = jnp.logical_and(lazy, u == 0)

        @pl.when(start)
        def _():
            load_w1.wait()

        xm = unit_rows(xs, u)
        for j in range(hidden // tile):
            cols = slice(j * tile, (j + 1) * tile)
            pre = dot(xm, w1[:, cols]).astype(BF16)
            us[u, :, cols] = pre
            uf = pre.astype(F32)
            tau = jnp.tanh(GELU_COEF * (uf + CUBIC_COEF * uf * uf * uf))
            ab[:, cols] = (0.5 * uf * (1.0 + tau)).astype(BF16)

        @pl.when(start)
        def _():
            load_w2.wait()

        products(0, u, ab[...], lambda m, h: dot(m, w2[:, h * half:(h + 1) * half]))

    def fwd_out(i):
        h0, h1 = final_sums(0, i)

        @pl.when(jnp.logical_not(last))
        def _():
            outs[0, i, :, :half] = h0
            outs[0, i, :, half:] = h1
            spread(0, i, outs.at[0, i], up, 0, False)

        @pl.when(last)
        def _():
            for h, v in ((0, h0), (1, h1)):
                cols = slice(h * half, (h + 1) * half)
                err = v.astype(F32) - tgt[i, :, cols].astype(F32)
                es[i, d, :, cols] = (err * scale).astype(BF16)
                err_acc[:, cols] += err * err
            spread(1, i, es.at[i, d], s, 0, True)

    def bwd_out(i):
        h0, h1 = final_sums(1, i)
        outs[1, i, :, :half] = h0
        outs[1, i, :, half:] = h1
        spread(1, i, outs.at[1, i], down, 1, False)

    def saved(which, j):
        src, dst = ((dw1, dw1_hbm), (dw2, dw2_hbm))[which]
        r = pl.ds(j * tile, tile)
        return pltpu.make_async_copy(src.at[r], dst.at[r], store_sem.at[which, j])

    def store(u, which, j):
        @pl.when(u == units - 1)
        def _():
            saved(which, j).start()

    def grad_out(u):
        em = unit_rows(es, u)
        for j in range(hidden // tile):
            r = slice(j * tile, (j + 1) * tile)
            dw2[r, :] += dot(ab[:, r], em, TN)
            store(u, 1, j)

    def grad_in(u):
        gm = gb[...]
        for j in range(width // tile):
            r = slice(j * tile, (j + 1) * tile)
            xt = xs[pl.ds(u * UNIT, UNIT), :, :, r].reshape(UNIT * tokens, tile)
            dw1[r, :] += dot(xt, gm, TN)
            store(u, 0, j)

    def bwd(u):
        for k in range(UNIT):
            arrived(1, u * UNIT + k)
        em = unit_rows(es, u)
        for j in range(hidden // tile):
            cols = slice(j * tile, (j + 1) * tile)
            q = dot(em, w2t[:, cols]).astype(BF16).astype(F32)
            uf = us[u, :, cols].astype(F32)
            sq = uf * uf
            tau = jnp.tanh(GELU_COEF * (uf + CUBIC_COEF * uf * sq))
            slope = 0.5 * (1.0 + tau) + 0.5 * uf * (1.0 - tau * tau) * GELU_COEF * (1.0 + 3.0 * CUBIC_COEF * sq)
            gb[:, cols] = (slope * q).astype(BF16)
            ab[:, cols] = (0.5 * uf * (1.0 + tau)).astype(BF16)

        @pl.when(jnp.logical_not(first))
        def _():
            products(1, u, gb[...], lambda m, h: dot(m, w1t[:, h * half:(h + 1) * half]))

    def op(name, f, lag, tick):
        u = tick - lag - (ahead if f else 0)
        live = jnp.logical_and(u >= 0, u < units)
        if name == "A":
            run = bwd if f else fwd
        elif name == "T":
            run = lambda u: transpose(u - 1)
            live = jnp.logical_and(lazy, jnp.logical_and(u >= 1, u <= pieces))
        elif name == "G2":
            run = grad_out
        elif name == "G1":
            run = grad_in
        else:
            step = {
                "E4": functools.partial(relay_sums, f),
                "E5": bwd_out if f else fwd_out,
            }[name]

            def each(k, c):
                step(u * UNIT + k)
                return c

            def run(u):
                lax.fori_loop(0, UNIT, each, 0)

        if f and name in ("E4", "E5"):
            live = jnp.logical_and(live, jnp.logical_not(first))

        @pl.when(live)
        def _():
            run(u)

    def tick(t, c):
        for name, f, lag in ORDER:
            op(name, f, lag, t)
        return c

    begin = min(lag for _, _, lag in ORDER)
    lax.fori_loop(begin, units + ahead + max(lag for _, f, lag in ORDER if f), tick, 0)

    @pl.when(last)
    def _():
        ltile[d] = jnp.full(ltile.shape[1:], 0.5 * jnp.sum(err_acc[...]), F32)
        for k in (2, 1, 3):
            send(ltile.at[d], ltile.at[d], l_sem.at[k], l_sem.at[n_model], peer(k), s).start()
        got(ltile.at[pl.ds(0, n_model - 1)], l_sem.at[n_model])
        ltile[n_model] = ltile[0] + ltile[1] + ltile[2] + ltile[3]
        for k in (1, 2, 3):
            sent(ltile.at[0], l_sem.at[k])

    @pl.when(jnp.logical_not(last))
    def _():
        got(ltile.at[n_model], chain_sem.at[0])

    for b in range(UNIT):
        sums_sent(0, b)
    peers = (1, 2, 3)
    for k in peers:
        sent(outs.at[0], o_sem.at[0, k])

    @pl.when(jnp.logical_not(last))
    def _():
        sent(outs.at[0], o_sem.at[0, 0])

    @pl.when(jnp.logical_not(first))
    def _():
        chain = send(ltile.at[n_model], ltile.at[n_model], chain_sem.at[1], chain_sem.at[0], d, down)
        chain.start()
        for b in range(UNIT):
            sums_sent(1, b)
        for k in (0, *peers):
            sent(outs.at[1], o_sem.at[1, k])
        chain.wait_send()

    loss_ref[0] = jnp.sum(ltile[n_model, 0:1, 0:1]) * scale
    for which in (0, 1):
        for j in range(hidden // tile):
            saved(which, j).wait()


def run_group(n_stage, tokens, x, t, w1, w2):
    num, n_model, rows, width = x.shape
    hidden = w1.shape[1]
    half = width // 2
    any_spec = pl.BlockSpec(memory_space=pl.ANY)
    vmem = pltpu.VMEM
    dma = pltpu.SemaphoreType.DMA
    flops = 12 * num * tokens * width * hidden
    return pl.pallas_call(
        functools.partial(kernel, n_stage),
        out_shape=(
            jax.ShapeDtypeStruct(w1.shape, F32),
            jax.ShapeDtypeStruct(w2.shape, F32),
            jax.ShapeDtypeStruct((1,), F32),
        ),
        in_specs=[any_spec] * 4,
        out_specs=(any_spec, any_spec, pl.BlockSpec(memory_space=pltpu.SMEM)),
        scratch_shapes=[
            vmem(w1.shape, BF16),
            vmem(w2.shape, BF16),
            vmem(w1.shape[::-1], BF16),
            vmem(w2.shape[::-1], BF16),
            vmem(w1.shape, F32),
            vmem(w2.shape, F32),
            vmem(x.shape, BF16),
            vmem((num // UNIT, UNIT * tokens, hidden), BF16),
            vmem(x.shape, BF16),
            vmem((UNIT * tokens, hidden), BF16),
            vmem((UNIT * tokens, hidden), BF16),
            vmem((2, 2, UNIT, n_model, rows, half), F32),
            vmem((2, SLOTS, 6, rows, half), F32),
            vmem((2, num, rows, width), BF16),
            vmem((rows, width), F32),
            vmem((n_model + 1, 8, 128), F32),
            dma((5,)),
            dma((2, num)),
            dma((2, SLOTS, 6)),
            dma((2, UNIT, 6)),
            dma((2, n_model)),
            dma((n_model + 1,)),
            dma((2,)),
            dma((2, 3)),
        ],
        compiler_params=pltpu.CompilerParams(
            collective_id=0, has_side_effects=True, vmem_limit_bytes=67043328
        ),
        cost_estimate=pl.CostEstimate(flops=flops, bytes_accessed=60 * width * hidden // 4, transcendentals=0),
        name="pipeline_step",
    )(x, t, w1, w2)


def solution(mesh):
    n_stage = mesh.shape["stage"]
    n_model = mesh.shape["model"]

    def stage_step(inputs, targets, w_in, w_out):
        width = inputs.shape[-1]
        total = inputs.shape[0] * inputs.shape[1]
        num = total // TOKENS
        shape = (num, n_model, TOKENS // n_model, width)
        dw1, dw2, loss = run_group(
            n_stage, TOKENS, inputs.reshape(shape), targets.reshape(shape), w_in[0, 0], w_out[0, 0])
        return dw1[None, None], dw2[None, None], loss

    return jax.shard_map(
        stage_step,
        mesh=mesh,
        in_specs=(P("data", None, None), P("data", None, None), P("stage", None, None, "model"), P("stage", None, "model", None)),
        out_specs=(P(("data", "stage"), None, None, "model"), P(("data", "stage"), None, "model", None), P("data")),
        check_vma=False,
    )
```

time: 734 us -> 567 us (0.77)
  Pallas kernels: 720 us -> 552 us
    pallas_call x1, Pallas kernels: 720 us -> 552 us  [run_group(): pl.pallas_call(functools.partial(kernel, n_stage), out_shape=(jax.ShapeDt...]
where the time goes in v2:
time: 567 us
  Pallas kernels  552 us (97%)
  local copies, waits for them, and re-layouts  12.3 us (2%)
    pallas_call x1, Pallas kernels, run_group(): pl.pallas_call(functools.partial(kernel, n_stage), out_shape=(jax.ShapeDt...  552 us
    unnamed x4, local copies, waits for them, and re-layouts  12.3 us

profile of v2, /device:TPU:96, one launch (start us, length us, event | category | flops | bytes accessed | tf_op | source)
XLA Modules:
  0.0 566.7 jit_solution(1198992111033745094)
XLA Ops:
  0.6 552.0 %pipeline_step.1 = (f32[1536,1536]{1,0:T(8,128)}, f32[1536,1536]{1,0:T(8,128)}, f32[1]{0:T(128)}) custom-call(bf16[32,4,16,1536]{3,2,1,0:T(8,128)(2,1)} %bitcast.8, bf16[32,4,16,1536]{3,2,1,0:T(8,128)(2,1)} %bitcast.9, bf16[1536,1536]{1,0:T(8,128)(2,1)} %bitcast.10, bf16[1536,1536]{1,0:T(8,128)(2,1)} %bitcast.11), custom_call_target="tpu_custom_call" | custom-call | flops 57982058496 | bytes 35389440 | tf_op jit(solution)/shard_map/pipeline_step/pallas_call | solution.py:393
  552.7 0.0 copy-start
  552.7 8.6 %copy.10 = f32[1,1,1536,1536]{3,2,1,0:T(8,128)} copy(f32[1,1,1536,1536]{3,2,1,0:T(8,128)} %bitcast.7) | data formatting | bytes 18874368
  561.3 0.0 copy-done
  561.3 3.7 copy.11
Async XLA Ops:
  552.7 8.6 %copy-start = (f32[1536,1536]{1,0:T(8,128)S(1)}, f32[1536,1536]{1,0:T(8,128)}, u32[]{:S(2)}) copy-start(f32[1536,1536]{1,0:T(8,128)} %get-tuple-element.7) | copy-start | bytes 28311556

commit v3 on v2

--- a/solution.py
+++ b/solution.py
@@ -15,9 +15,10 @@
 
 TOKENS = 64
 UNIT = 2
+RING = 8
 SLOTS = 2 * UNIT
 AHEAD = (22, 19, 16, 13, 10, 7, 4, 1)
-ORDER = (("A", 0, 0), ("T", 0, 0), ("E5", 1, 1), ("E4", 0, 0), ("A", 1, 0), ("E5", 0, 0), ("G2", 1, 0), ("G1", 1, 0), ("E4", 1, 0))
+ORDER = (("A", 0, 0), ("T", 0, 0), ("E5", 1, 1), ("E4", 0, 0), ("A", 1, 0), ("G2", 1, 0), ("E5", 0, 0), ("G1", 1, 0), ("E4", 1, 0))
 TN = (((0,), (0,)), ((), ()))
 
 
@@ -25,9 +26,9 @@
     return lax.dot_general(a, b, dims, preferred_element_type=F32)
 
 
-def kernel(n_stage, x_hbm, t_hbm, w1_hbm, w2_hbm, dw1_hbm, dw2_hbm, loss_ref,
-           w1, w2, w1t, w2t, dw1, dw2, xs, us, es, ab, gb, ps, rs, outs, err_acc, ltile,
-           load_sem, in_sem, r_sem, p_sem, o_sem, l_sem, chain_sem, store_sem):
+def kernel(n_stage, x_hbm, t_hbm, w1_hbm, w2_hbm, dw1, dw2, loss_ref,
+           w1, w2, w1t, w2t, xs, us, es, ab, gb, ps, rs, outs, back, err_acc, ltile,
+           load_sem, in_sem, r_sem, p_sem, o_sem, back_sem, l_sem, chain_sem):
     n_model = 4
     num, _, rows, width = xs.shape
     tokens = n_model * rows
@@ -64,7 +65,7 @@
         send(ref, ref, sem, sem, right, s).wait_send()
 
     units = num // UNIT
-    tgt = outs.at[0]
+    tgt = outs
     load_w1 = pltpu.make_async_copy(w1_hbm, w1, load_sem.at[0])
     load_w2 = pltpu.make_async_copy(w2_hbm, w2, load_sem.at[1])
     load_x0 = pltpu.make_async_copy(x_hbm.at[pl.ds(0, UNIT)], xs.at[pl.ds(0, UNIT)], load_sem.at[2])
@@ -178,10 +179,10 @@
         h1 = base[:, half:].astype(F32) + (ps[f, 1, b, d] + rs[f, slot, 2] + rs[f, slot, 5])
         return h0.astype(BF16), h1.astype(BF16)
 
-    def spread(f, i, src, stage, sender, here):
+    def spread(f, i, src, stage, here):
         dst = acts[f].at[i, d]
         for k in (2, 1, 3) if here else (2, 1, 3, 0):
-            send(src, dst, o_sem.at[sender, k], in_sem.at[f, i], peer(k), stage).start()
+            send(src, dst, o_sem.at[k], in_sem.at[f, i], peer(k), stage).start()
 
     def arrived(f, i):
         if f:
@@ -236,45 +237,41 @@
         products(0, u, ab[...], lambda m, h: dot(m, w2[:, h * half:(h + 1) * half]))
 
     def fwd_out(i):
-        h0, h1 = final_sums(0, i)
+        ha, hb = final_sums(0, i)
 
         @pl.when(jnp.logical_not(last))
         def _():
-            outs[0, i, :, :half] = h0
-            outs[0, i, :, half:] = h1
-            spread(0, i, outs.at[0, i], up, 0, False)
+            outs[i, :, :half] = ha
+            outs[i, :, half:] = hb
+            spread(0, i, outs.at[i], up, False)
 
         @pl.when(last)
         def _():
-            for h, v in ((0, h0), (1, h1)):
+            for h, v in ((0, ha), (1, hb)):
                 cols = slice(h * half, (h + 1) * half)
                 err = v.astype(F32) - tgt[i, :, cols].astype(F32)
                 es[i, d, :, cols] = (err * scale).astype(BF16)
                 err_acc[:, cols] += err * err
-            spread(1, i, es.at[i, d], s, 0, True)
+            spread(1, i, es.at[i, d], s, True)
 
     def bwd_out(i):
-        h0, h1 = final_sums(1, i)
-        outs[1, i, :, :half] = h0
-        outs[1, i, :, half:] = h1
-        spread(1, i, outs.at[1, i], down, 1, False)
-
-    def saved(which, j):
-        src, dst = ((dw1, dw1_hbm), (dw2, dw2_hbm))[which]
-        r = pl.ds(j * tile, tile)
-        return pltpu.make_async_copy(src.at[r], dst.at[r], store_sem.at[which, j])
-
-    def store(u, which, j):
-        @pl.when(u == units - 1)
-        def _():
-            saved(which, j).start()
+        ha, hb = final_sums(1, i)
+        slot = lax.rem(i, RING)
+
+        @pl.when(i >= RING)
+        def _():
+            sent(back.at[pl.ds(0, n_model)], back_sem.at[slot])
+
+        back[slot, :, :half] = ha
+        back[slot, :, half:] = hb
+        for k in (2, 1, 3, 0):
+            send(back.at[slot], es.at[i, d], back_sem.at[slot], in_sem.at[1, i], peer(k), down).start()
 
     def grad_out(u):
         em = unit_rows(es, u)
         for j in range(hidden // tile):
             r = slice(j * tile, (j + 1) * tile)
             dw2[r, :] += dot(ab[:, r], em, TN)
-            store(u, 1, j)
 
     def grad_in(u):
         gm = gb[...]
@@ -282,7 +279,6 @@
             r = slice(j * tile, (j + 1) * tile)
             xt = xs[pl.ds(u * UNIT, UNIT), :, :, r].reshape(UNIT * tokens, tile)
             dw1[r, :] += dot(xt, gm, TN)
-            store(u, 0, j)
 
     def bwd(u):
         for k in range(UNIT):
@@ -360,11 +356,11 @@
         sums_sent(0, b)
     peers = (1, 2, 3)
     for k in peers:
-        sent(outs.at[0], o_sem.at[0, k])
+        sent(outs, o_sem.at[k])
 
     @pl.when(jnp.logical_not(last))
     def _():
-        sent(outs.at[0], o_sem.at[0, 0])
+        sent(outs, o_sem.at[0])
 
     @pl.when(jnp.logical_not(first))
     def _():
@@ -372,14 +368,11 @@
         chain.start()
         for b in range(UNIT):
             sums_sent(1, b)
-        for k in (0, *peers):
-            sent(outs.at[1], o_sem.at[1, k])
+        for slot in range(RING):
+            sent(back.at[pl.ds(0, n_model)], back_sem.at[slot])
         chain.wait_send()
 
     loss_ref[0] = jnp.sum(ltile[n_model, 0:1, 0:1]) * scale
-    for which in (0, 1):
-        for j in range(hidden // tile):
-            saved(which, j).wait()
 
 
 def run_group(n_stage, tokens, x, t, w1, w2):
@@ -393,19 +386,17 @@
     return pl.pallas_call(
         functools.partial(kernel, n_stage),
         out_shape=(
-            jax.ShapeDtypeStruct(w1.shape, F32),
-            jax.ShapeDtypeStruct(w2.shape, F32),
+            vmem(w1.shape, F32),
+            vmem(w2.shape, F32),
             jax.ShapeDtypeStruct((1,), F32),
         ),
         in_specs=[any_spec] * 4,
-        out_specs=(any_spec, any_spec, pl.BlockSpec(memory_space=pltpu.SMEM)),
+        out_specs=(pl.BlockSpec(memory_space=vmem), pl.BlockSpec(memory_space=vmem), pl.BlockSpec(memory_space=pltpu.SMEM)),
         scratch_shapes=[
             vmem(w1.shape, BF16),
             vmem(w2.shape, BF16),
             vmem(w1.shape[::-1], BF16),
             vmem(w2.shape[::-1], BF16),
-            vmem(w1.shape, F32),
-            vmem(w2.shape, F32),
             vmem(x.shape, BF16),
             vmem((num // UNIT, UNIT * tokens, hidden), BF16),
             vmem(x.shape, BF16),
@@ -413,20 +404,21 @@
             vmem((UNIT * tokens, hidden), BF16),
             vmem((2, 2, UNIT, n_model, rows, half), F32),
             vmem((2, SLOTS, 6, rows, half), F32),
-            vmem((2, num, rows, width), BF16),
+            vmem((num, rows, width), BF16),
+            vmem((RING, rows, width), BF16),
             vmem((rows, width), F32),
             vmem((n_model + 1, 8, 128), F32),
             dma((5,)),
             dma((2, num)),
             dma((2, SLOTS, 6)),
             dma((2, UNIT, 6)),
-            dma((2, n_model)),
+            dma((n_model,)),
+            dma((RING,)),
             dma((n_model + 1,)),
             dma((2,)),
-            dma((2, 3)),
         ],
         compiler_params=pltpu.CompilerParams(
-            collective_id=0, has_side_effects=True, vmem_limit_bytes=67043328
+            collective_id=0, has_side_effects=True, vmem_limit_bytes=48000000
         ),
         cost_estimate=pl.CostEstimate(flops=flops, bytes_accessed=60 * width * hidden // 4, transcendentals=0),
         name="pipeline_step",

time: 567 us -> 556 us (0.981)
  Pallas kernels: 552 us -> 546 us
    pallas_call x1, Pallas kernels: 552 us -> 546 us  [run_group(): pl.pallas_call(functools.partial(kernel, n_stage), out_shape=(vmem(w1.sha...]
    unnamed x4 -> x2, local copies, waits for them, and re-layouts: 12.3 us -> 7.49 us
where the time goes in v3:
time: 556 us
  Pallas kernels  546 us (98%)
  local copies, waits for them, and re-layouts  7.49 us (1%)
    pallas_call x1, Pallas kernels, run_group(): pl.pallas_call(functools.partial(kernel, n_stage), out_shape=(vmem(w1.sha...  546 us

profile of v3, /device:TPU:96, one launch (start us, length us, event | category | flops | bytes accessed | tf_op | source)
XLA Modules:
  0.0 556.0 jit_solution(16898990183935862112)
XLA Ops:
  0.6 546.2 %pipeline_step.1 = (f32[1536,1536]{1,0:T(8,128)S(1)}, f32[1536,1536]{1,0:T(8,128)S(1)}, f32[1]{0:T(128)}) custom-call(bf16[32,4,16,1536]{3,2,1,0:T(8,128)(2,1)} %bitcast.8, bf16[32,4,16,1536]{3,2,1,0:T(8,128)(2,1)} %bitcast.9, bf16[1536,1536]{1,0:T(8,128)(2,1)} %bitcast.10, bf16[1536,1536]{1,0:T(8,128)(2,1)} %bitcast.11), custom_call_target="tpu_custom_call" | custom-call | flops 57982058496 | bytes 35389440 | tf_op jit(solution)/shard_map/pipeline_step/pallas_call | solution.py:386
  546.9 3.7 copy.10
  550.6 3.7 copy.11
